TPU v7x, 256 devices: a whole 4x4x8 slice. The times are simulated.
256 devices in a mesh: bank: 8 (over y, x_lo), zero: 32 (over z, x_hi, core).
Axes of the slice: x: 4 (x_hi: 2, x_lo: 2; x = x_hi * 2 + x_lo), y: 4, z: 8, core: 2. Of those that a mesh axis runs over, the one named last changes fastest.
Arguments:
- master_gate: float32 [64, 2048, 1024], P('bank', 'zero'), may hold values from -0.25 to 0.25
- master_up: float32 [64, 2048, 1024], P('bank', 'zero'), may hold values from -0.25 to 0.25
- master_down: float32 [64, 1024, 2048], P('bank', None, 'zero'), may hold values from -0.375 to 0.375
- router_weight: float32 [2048, 64], P('zero', 'bank'), may hold values from -0.125 to 0.125
- router_gain: float32 [2048], P('zero'), may hold values from 0.25 to 1.75
Outputs:
- final_gate: bfloat16 [64, 2048, 1024], P('bank', None, 'zero')
- final_up: bfloat16 [64, 2048, 1024], P('bank', None, 'zero')
- final_down: bfloat16 [64, 1024, 2048], P('bank', 'zero')
- scale_gate: float32 [64, 1024], P('bank', 'zero')
- scale_up: float32 [64, 1024], P('bank', 'zero')
- scale_down: float32 [64, 1024], P('bank', 'zero')
- serve_router: bfloat16 [2048, 64], replicated
All inputs are finite; a program needn't handle non-finite values.
Results may differ from a plain program's by a relative error of at most 0.0085.
Values may be sent and summed in bfloat16 or wider, within the bound.
A program may use at most 64 MiB of HBM per device.

v0:
```python
import jax
import jax.numpy as jnp
from jax import lax
from jax.sharding import PartitionSpec as P


def from_everyone(value, axis):
    copies = jnp.broadcast_to(value, (lax.axis_size(axis), *value.shape))
    return lax.all_to_all(copies, axis, split_axis=0, concat_axis=0, tiled=True)


def over_copies(value, axis):
    everything = from_everyone(value, axis)
    return jnp.sum(everything.astype(jnp.float32), axis=0)


def sent_together(arrays, axis, split_dim, concat_dim, along):
    both = jnp.concatenate(arrays, axis=along)
    whole, at, gathered = (
        lax.all_to_all(both, axis, split_axis=split_dim, concat_axis=concat_dim, tiled=True),
        0,
        [],
    )
    for a in arrays:
        gathered.append(lax.slice_in_dim(whole, at, at + a.shape[along], axis=along))
        at += a.shape[along]
    return tuple(gathered)


def laid_out(tiles, dim):
    lengths = list(tiles.shape[1:])
    lengths[dim] *= tiles.shape[0]
    return jnp.moveaxis(tiles, 0, dim).reshape(lengths)


def gathered_copies(value, axis, dim):
    tiles = from_everyone(value, axis)
    return laid_out(tiles, dim)


def local(master_gate, master_up, master_down, router_weight, router_gain):
    total_gate, total_up, total_down = (
        over_copies(jnp.sum(master_gate * master_gate, axis=1).astype(jnp.bfloat16), "zero").astype(
            jnp.float32
        ),
        over_copies(jnp.sum(master_up * master_up, axis=1).astype(jnp.bfloat16), "zero").astype(
            jnp.float32
        ),
        over_copies(jnp.sum(master_down * master_down, axis=2).astype(jnp.bfloat16), "zero").astype(
            jnp.float32
        ),
    )
    scale_gate = jnp.sqrt(total_gate)
    scale_up = jnp.sqrt(total_up)
    scale_down = jnp.sqrt(total_down)
    narrow_gate, narrow_up, narrow_down = (
        (master_gate / jnp.expand_dims(scale_gate, 1)).astype(jnp.bfloat16),
        (master_up / jnp.expand_dims(scale_up, 1)).astype(jnp.bfloat16),
        (master_down / jnp.expand_dims(scale_down, 2)).astype(jnp.bfloat16),
    )
    final_gate, final_up = sent_together((narrow_gate, narrow_up), "zero", 2, 1, 0)
    final_down = lax.all_to_all(narrow_down, "zero", split_axis=1, concat_axis=2, tiled=True)
    scale_gate = lax.dynamic_slice_in_dim(
        scale_gate, lax.axis_index("zero") * final_gate.shape[2], final_gate.shape[2], axis=1
    )
    scale_up = lax.dynamic_slice_in_dim(
        scale_up, lax.axis_index("zero") * final_up.shape[2], final_up.shape[2], axis=1
    )
    scale_down = lax.dynamic_slice_in_dim(
        scale_down, lax.axis_index("zero") * final_down.shape[1], final_down.shape[1], axis=1
    )
    part_router = (router_weight * router_gain[:, None]).astype(jnp.bfloat16)
    row_router = gathered_copies(part_router, "zero", 0)
    serve_router = gathered_copies(row_router, "bank", 1)
    return (final_gate, final_up, final_down, scale_gate, scale_up, scale_down, serve_router)


def solution(mesh):
    in_specs = (
        P("bank", "zero", None),
        P("bank", "zero", None),
        P("bank", None, "zero"),
        P("zero", "bank"),
        P("zero"),
    )
    out_specs = (
        P("bank", None, "zero"),
        P("bank", None, "zero"),
        P("bank", "zero", None),
        P("bank", "zero"),
        P("bank", "zero"),
        P("bank", "zero"),
        P(),
    )
    return jax.shard_map(local, mesh=mesh, in_specs=in_specs, out_specs=out_specs, check_vma=False)
```

profile of v0, /device:TPU:1, one launch (start us, length us, event | category | flops | bytes accessed | tf_op | source)
XLA Modules:
  0.0 214.5 jit_solution(11568245509490080332)
XLA Ops:
  0.6 0.7 multiply_convert_fusion
  1.5 22.0 %all_to_all.58 = bf16[32,2,256]{2,1,0:T(2,128)(2,1)S(1)} all-to-all(bf16[32,2,256]{2,1,0:T(2,128)(2,1)S(1)} %reshape.38), channel_id=1, replica_groups=mesh['bank'=8,'zero'=32] {'zero'}, dimensions={0} | all-to-all | bytes 65536 | tf_op jit(solution)/shard_map/all_to_all | solution.py:9
  23.6 0.1 reshape.32
  23.7 0.7 broadcast_in_dim.23
  24.4 4.4 %all-to-all-start.6 = ((bf16[8,2048,8]{1,2,0:T(8,128)(2,1)}), bf16[8,2048,8]{1,2,0:T(8,128)(2,1)S(1)}, u32[]{:S(2)}, u32[]{:S(2)}) async-start(bf16[8,2048,8]{1,2,0:T(8,128)(2,1)} %broadcast_in_dim.23), calls=%async_computation.6 | async-start | bytes 524288 | tf_op jit(solution)/shard_map/all_to_all | solution.py:9
  28.8 1.9 multiply_reduce_fusion
  30.7 4.8 %all-to-all-done.6 = bf16[8,2048,8]{1,2,0:T(8,128)(2,1)S(1)} async-done(((bf16[8,2048,8]{1,2,0:T(8,128)(2,1)}), bf16[8,2048,8]{1,2,0:T(8,128)(2,1)S(1)}, u32[]{:S(2)}, u32[]{:S(2)}) %all-to-all-start.6) | async-done | bytes 262176 | tf_op jit(solution)/shard_map/all_to_all | solution.py:9
  35.5 0.9 broadcast_in_dim.21
  36.4 5.1 %all-to-all-start.3 = ((bf16[32,8,1024]{2,1,0:T(8,128)(2,1)}), bf16[32,8,1024]{2,1,0:T(8,128)(2,1)S(1)}, u32[]{:S(2)}, u32[]{:S(2)}) async-start(bf16[32,8,1024]{2,1,0:T(8,128)(2,1)} %broadcast_in_dim.21), calls=%async_computation.3 | async-start | bytes 1048576 | tf_op jit(solution)/shard_map/all_to_all | solution.py:9
  41.4 0.3 multiply_reduce_fusion.1
  41.7 17.0 %all-to-all-done.3 = bf16[32,8,1024]{2,1,0:T(8,128)(2,1)S(1)} async-done(((bf16[32,8,1024]{2,1,0:T(8,128)(2,1)}), bf16[32,8,1024]{2,1,0:T(8,128)(2,1)S(1)}, u32[]{:S(2)}, u32[]{:S(2)}) %all-to-all-start.3) | async-done | bytes 524320 | tf_op jit(solution)/shard_map/all_to_all | solution.py:9
  58.7 0.9 broadcast_in_dim.20
  59.6 5.5 %all-to-all-start.1 = ((bf16[32,8,1024]{2,1,0:T(8,128)(2,1)}), bf16[32,8,1024]{2,1,0:T(8,128)(2,1)S(1)}, u32[]{:S(2)}, u32[]{:S(2)}) async-start(bf16[32,8,1024]{2,1,0:T(8,128)(2,1)} %broadcast_in_dim.20), calls=%async_computation.1 | async-start | bytes 1048576 | tf_op jit(solution)/shard_map/all_to_all | solution.py:9
  65.1 2.0 multiply_reduce_fusion.2
  67.1 14.8 %all-to-all-done.1 = bf16[32,8,1024]{2,1,0:T(8,128)(2,1)S(1)} async-done(((bf16[32,8,1024]{2,1,0:T(8,128)(2,1)}), bf16[32,8,1024]{2,1,0:T(8,128)(2,1)S(1)}, u32[]{:S(2)}, u32[]{:S(2)}) %all-to-all-start.1) | async-done | bytes 524320 | tf_op jit(solution)/shard_map/all_to_all | solution.py:9
  81.9 0.9 broadcast_in_dim.19
  82.8 5.9 %all-to-all-start = ((bf16[32,8,1024]{2,1,0:T(8,128)(2,1)}), bf16[32,8,1024]{2,1,0:T(8,128)(2,1)}, u32[]{:S(2)}, u32[]{:S(2)}) async-start(bf16[32,8,1024]{2,1,0:T(8,128)(2,1)} %broadcast_in_dim.19), calls=%async_computation | async-start | bytes 1048576 | tf_op jit(solution)/shard_map/all_to_all | solution.py:9
  88.7 2.7 %copy.54 = f32[8,1024,64]{2,0,1:T(8,128)} copy(f32[8,1024,64]{1,2,0:T(8,128)S(1)} %copy-done) | data formatting | bytes 4194304 | tf_op args[2]
  91.6 0.2 copy.53
  91.8 3.9 %fusion.2 = bf16[1024,8,64]{2,1,0:T(8,128)(2,1)} fusion(f32[8,1024,64]{2,0,1:T(8,128)} %copy.54, f32[8,1024]{0,1:T(8,128)S(1)} %copy.53), kind=kLoop, calls=%fused_computation.16 | loop fusion | flops 1048576 | bytes 3178496
  95.6 4.8 %reshape.36 = bf16[32,2,8192]{2,1,0:T(2,128)(2,1)} reshape(bf16[1024,8,64]{2,1,0:T(8,128)(2,1)} %fusion.2) | data formatting | bytes 2097152
  100.4 5.2 %all-to-all-done = bf16[32,8,1024]{2,1,0:T(8,128)(2,1)} async-done(((bf16[32,8,1024]{2,1,0:T(8,128)(2,1)}), bf16[32,8,1024]{2,1,0:T(8,128)(2,1)}, u32[]{:S(2)}, u32[]{:S(2)}) %all-to-all-start) | async-done | bytes 524320 | tf_op jit(solution)/shard_map/all_to_all | solution.py:9
  105.6 5.8 %all-to-all-start.4 = ((bf16[32,2,8192]{2,1,0:T(2,128)(2,1)}), bf16[32,2,8192]{2,1,0:T(2,128)(2,1)S(1)}, u32[]{:S(2)}, u32[]{:S(2)}) async-start(bf16[32,2,8192]{2,1,0:T(2,128)(2,1)} %reshape.36), calls=%async_computation.4 | async-start | bytes 2097152 | tf_op jit(solution)/shard_map/all_to_all | solution.py:62
  111.4 2.8 %copy.47 = f32[8,64,1024]{1,0,2:T(8,128)} copy(f32[8,64,1024]{2,1,0:T(8,128)S(1)} %copy-done.1) | data formatting | bytes 4194304 | tf_op args[0]
  114.2 3.9 %copy.49 = f32[8,64,1024]{1,0,2:T(8,128)} copy(f32[8,64,1024]{2,1,0:T(8,128)} %param.6) | data formatting | bytes 4194304 | tf_op args[1]
  118.2 1.1 convert_reduce_fusion.2
  119.3 0.2 copy.46
  119.5 0.2 copy.48
  119.8 6.2 %divide_convert_fusion.1 = (bf16[8,64,1024]{1,0,2:T(8,128)(2,1)S(1)}, bf16[8,64,1024]{1,0,2:T(8,128)(2,1)S(1)}) fusion(f32[8,64,1024]{1,0,2:T(8,128)} %copy.49, f32[8,1024]{0,1:T(8,128)S(1)} %copy.48, f32[8,64,1024]{1,0,2:T(8,128)} %copy.47, f32[8,1024]{0,1:T(8,128)S(1)} %copy.46), kind=kLoop, calls=%fused_computation.2 | loop fusion | flops 2097152 | bytes 6356992 | tf_op jit(solution)/shard_map/convert_element_type | solution.py:58
  126.0 2.9 %fusion.1 = bf16[1024,16,64]{2,1,0:T(8,128)(2,1)} fusion(bf16[8,64,1024]{1,0,2:T(8,128)(2,1)S(1)} %get-tuple-element.9, bf16[8,64,1024]{1,0,2:T(8,128)(2,1)S(1)} %get-tuple-element.10), kind=kLoop, calls=%fused_computation.15 | loop fusion | flops 4194304 | bytes 4194304
  128.8 7.9 %reshape.34 = bf16[32,2,16384]{2,1,0:T(2,128)(2,1)} reshape(bf16[1024,16,64]{2,1,0:T(8,128)(2,1)} %fusion.1) | data formatting | bytes 4194304
  136.7 2.8 %all-to-all-done.4 = bf16[32,2,8192]{2,1,0:T(2,128)(2,1)S(1)} async-done(((bf16[32,2,8192]{2,1,0:T(2,128)(2,1)}), bf16[32,2,8192]{2,1,0:T(2,128)(2,1)S(1)}, u32[]{:S(2)}, u32[]{:S(2)}) %all-to-all-start.4) | async-done | bytes 1048608 | tf_op jit(solution)/shard_map/all_to_all | solution.py:62
  139.5 7.0 %all-to-all-start.2 = ((bf16[32,2,16384]{2,1,0:T(2,128)(2,1)}), bf16[32,2,16384]{2,1,0:T(2,128)(2,1)S(1)}, u32[]{:S(2)}, u32[]{:S(2)}) async-start(bf16[32,2,16384]{2,1,0:T(2,128)(2,1)} %reshape.34), calls=%async_computation.2 | async-start | bytes 4194304 | tf_op jit(solution)/shard_map/all_to_all | solution.py:20
  146.5 0.7 constant_dynamic-slice_fusion
  147.2 0.7 constant_dynamic-slice_fusion.1
  147.8 0.7 constant_dynamic-slice_fusion.2
  148.5 2.4 %reshape.37 = bf16[1024,8,64]{2,1,0:T(8,128)(2,1)} reshape(bf16[32,2,8192]{2,1,0:T(2,128)(2,1)S(1)} %all-to-all-done.4) | data formatting | bytes 2097152
  150.8 4.2 %copy.56 = bf16[8,32,32,64]{3,2,1,0:T(8,128)(2,1)} copy(bf16[8,32,32,64]{3,0,1,2:T(8,128)(2,1)} %bitcast.32) | data formatting | bytes 2097152 | tf_op jit(solution)/shard_map/all_to_all | solution.py:62
  155.1 4.2 %all_to_all.48 = bf16[8,32,2048]{2,1,0:T(8,128)(2,1)} reshape(bf16[8,32,32,64]{3,2,1,0:T(8,128)(2,1)} %copy.56) | data formatting | bytes 2097152 | tf_op jit(solution)/shard_map/all_to_all | solution.py:62
  159.3 37.1 %all-to-all-done.2 = bf16[32,2,16384]{2,1,0:T(2,128)(2,1)S(1)} async-done(((bf16[32,2,16384]{2,1,0:T(2,128)(2,1)}), bf16[32,2,16384]{2,1,0:T(2,128)(2,1)S(1)}, u32[]{:S(2)}, u32[]{:S(2)}) %all-to-all-start.2) | async-done | bytes 2097184 | tf_op jit(solution)/shard_map/all_to_all | solution.py:20
  196.4 4.0 %reshape.35 = bf16[1024,16,64]{2,1,0:T(8,128)(2,1)} reshape(bf16[32,2,16384]{2,1,0:T(2,128)(2,1)S(1)} %all-to-all-done.2) | data formatting | bytes 4194304
  200.4 3.3 %copy.50 = bf16[16,64,1024]{1,2,0:T(8,128)(2,1)S(1)} copy(bf16[16,64,1024]{1,0,2:T(8,128)(2,1)} %bitcast.31) | data formatting | bytes 4194304 | tf_op jit(solution)/shard_map/all_to_all | solution.py:20
  203.6 2.1 fusion
  205.7 0.8 copy.51
  206.5 2.4 %slice.13 = bf16[8,2048,32]{1,2,0:T(8,128)(2,1)} reshape(bf16[8,32,64,32]{2,1,3,0:T(8,128)(2,1)S(1)} %copy.51) | data formatting | bytes 2097152 | tf_op jit(solution)/shard_map/slice | solution.py:25
  209.0 2.4 %copy.52 = bf16[8,32,64,32]{2,1,3,0:T(8,128)(2,1)S(1)} copy(bf16[8,32,64,32]{2,3,1,0:T(8,128)(2,1)} %get-tuple-element.7) | data formatting | bytes 2097152 | tf_op jit(solution)/shard_map/slice | solution.py:25
  211.4 2.4 %slice.15 = bf16[8,2048,32]{1,2,0:T(8,128)(2,1)} reshape(bf16[8,32,64,32]{2,1,3,0:T(8,128)(2,1)S(1)} %copy.52) | data formatting | bytes 2097152 | tf_op jit(solution)/shard_map/slice | solution.py:25
  213.8 0.7 copy.60
  (19 shorter events, 0.5 us)
Async XLA Ops:
  24.4 17.0 %copy-start.2 = (f32[8,64,1024]{2,1,0:T(8,128)S(1)}, f32[8,64,1024]{2,1,0:T(8,128)}, u32[]{:S(2)}) copy-start(f32[8,64,1024]{2,1,0:T(8,128)} %param.6) | copy-start | bytes 6291460
  24.4 11.0 %all-to-all-start.6 = ((bf16[8,2048,8]{1,2,0:T(8,128)(2,1)}), bf16[8,2048,8]{1,2,0:T(8,128)(2,1)S(1)}, u32[]{:S(2)}, u32[]{:S(2)}) async-start(bf16[8,2048,8]{1,2,0:T(8,128)(2,1)} %broadcast_in_dim.23), calls=%async_computation.6 | async-start | bytes 524288 | tf_op jit(solution)/shard_map/all_to_all | solution.py:9
  36.4 22.4 %all-to-all-start.3 = ((bf16[32,8,1024]{2,1,0:T(8,128)(2,1)}), bf16[32,8,1024]{2,1,0:T(8,128)(2,1)S(1)}, u32[]{:S(2)}, u32[]{:S(2)}) async-start(bf16[32,8,1024]{2,1,0:T(8,128)(2,1)} %broadcast_in_dim.21), calls=%async_computation.3 | async-start | bytes 1048576 | tf_op jit(solution)/shard_map/all_to_all | solution.py:9
  59.6 22.3 %all-to-all-start.1 = ((bf16[32,8,1024]{2,1,0:T(8,128)(2,1)}), bf16[32,8,1024]{2,1,0:T(8,128)(2,1)S(1)}, u32[]{:S(2)}, u32[]{:S(2)}) async-start(bf16[32,8,1024]{2,1,0:T(8,128)(2,1)} %broadcast_in_dim.20), calls=%async_computation.1 | async-start | bytes 1048576 | tf_op jit(solution)/shard_map/all_to_all | solution.py:9
  65.1 23.6 %copy-start = (f32[8,1024,64]{1,2,0:T(8,128)S(1)}, f32[8,1024,64]{1,2,0:T(8,128)}, u32[]{:S(2)}) copy-start(f32[8,1024,64]{1,2,0:T(8,128)} %param.7) | copy-start | bytes 6291460
  81.9 9.5 %copy-start.3 = (bf16[32,8,1024]{2,1,0:T(8,128)(2,1)}, bf16[32,8,1024]{2,1,0:T(8,128)(2,1)S(1)}, u32[]{:S(2)}) copy-start(bf16[32,8,1024]{2,1,0:T(8,128)(2,1)S(1)} %all-to-all-done.1) | copy-start | bytes 1572868
  82.8 22.8 %all-to-all-start = ((bf16[32,8,1024]{2,1,0:T(8,128)(2,1)}), bf16[32,8,1024]{2,1,0:T(8,128)(2,1)}, u32[]{:S(2)}, u32[]{:S(2)}) async-start(bf16[32,8,1024]{2,1,0:T(8,128)(2,1)} %broadcast_in_dim.19), calls=%async_computation | async-start | bytes 1048576 | tf_op jit(solution)/shard_map/all_to_all | solution.py:9
  95.6 15.8 %copy-start.1 = (f32[8,64,1024]{2,1,0:T(8,128)S(1)}, f32[8,64,1024]{2,1,0:T(8,128)}, u32[]{:S(2)}) copy-start(f32[8,64,1024]{2,1,0:T(8,128)} %param.5) | copy-start | bytes 6291460
  105.6 33.9 %all-to-all-start.4 = ((bf16[32,2,8192]{2,1,0:T(2,128)(2,1)}), bf16[32,2,8192]{2,1,0:T(2,128)(2,1)S(1)}, u32[]{:S(2)}, u32[]{:S(2)}) async-start(bf16[32,2,8192]{2,1,0:T(2,128)(2,1)} %reshape.36), calls=%async_computation.4 | async-start | bytes 2097152 | tf_op jit(solution)/shard_map/all_to_all | solution.py:62
  114.2 3.9 %copy-start.4 = (bf16[32,8,1024]{2,1,0:T(8,128)(2,1)S(1)}, bf16[32,8,1024]{2,1,0:T(8,128)(2,1)}, u32[]{:S(2)}) copy-start(bf16[32,8,1024]{2,1,0:T(8,128)(2,1)} %copy-done.3) | copy-start | bytes 1572868
  139.5 56.9 %all-to-all-start.2 = ((bf16[32,2,16384]{2,1,0:T(2,128)(2,1)}), bf16[32,2,16384]{2,1,0:T(2,128)(2,1)S(1)}, u32[]{:S(2)}, u32[]{:S(2)}) async-start(bf16[32,2,16384]{2,1,0:T(2,128)(2,1)} %reshape.34), calls=%async_computation.2 | async-start | bytes 4194304 | tf_op jit(solution)/shard_map/all_to_all | solution.py:20
where the time goes:
time: 216 us; the launch traced here: 214 us
  waiting for transfers between devices  81.7 us (38%)
  local copies, waits for them, and re-layouts  57.3 us (27%)
  starting transfers between devices  33.5 us (16%)
  blocking collectives  22 us (10%)
  other arithmetic  19.1 us (9%)
    all_to_all x4, waiting for transfers between devices, from_everyone(): return lax.all_to_all(copies, axis, split_axis=0, concat_axis=0, tiled=True)  41.8 us
    all_to_all x1, waiting for transfers between devices, sent_together(): lax.all_to_all(both, axis, split_axis=split_dim, concat_axis=concat_dim,...  37.1 us
    unnamed x21, local copies, waits for them, and re-layouts  29.3 us
    all_to_all x1, blocking collectives, from_everyone(): return lax.all_to_all(copies, axis, split_axis=0, concat_axis=0, tiled=True)  22 us
    all_to_all x4, starting transfers between devices, from_everyone(): return lax.all_to_all(copies, axis, split_axis=0, concat_axis=0, tiled=True)  20.8 us
    slice x5, local copies, waits for them, and re-layouts, sent_together(): lax.slice_in_dim(whole, at, at + a.shape[along], axis=along)  10.1 us
    all_to_all x2, local copies, waits for them, and re-layouts, local(): lax.all_to_all(narrow_down, 'zero', split_axis=1, concat_axis=2, tiled=True)  8.47 us
    all_to_all x1, starting transfers between devices, sent_together(): lax.all_to_all(both, axis, split_axis=split_dim, concat_axis=concat_dim,...  6.96 us
  transfers between devices with their start and end apart: 6, of which 6 were waited for; matrix products, arithmetic and copies ran while one was open for 23% of the time, Pallas kernels for 0%

commit v1 on v0

--- a/solution.py
+++ b/solution.py
@@ -59,7 +59,12 @@
         (master_down / jnp.expand_dims(scale_down, 2)).astype(jnp.bfloat16),
     )
     final_gate, final_up = sent_together((narrow_gate, narrow_up), "zero", 2, 1, 0)
-    final_down = lax.all_to_all(narrow_down, "zero", split_axis=1, concat_axis=2, tiled=True)
+    final_down = jnp.concatenate(
+        lax.all_to_all(
+            jnp.stack(jnp.split(narrow_down, lax.axis_size("zero"), axis=1)), "zero", 0, 0
+        ),
+        axis=2,
+    )
     scale_gate = lax.dynamic_slice_in_dim(
         scale_gate, lax.axis_index("zero") * final_gate.shape[2], final_gate.shape[2], axis=1
     )

time: 216 us -> 226 us (1.046)
  blocking collectives: 22 us -> 0 us
  local copies, waits for them, and re-layouts: 57.3 us -> 78.7 us
  starting transfers between devices: 33.5 us -> 44.7 us
    all_to_all x1 -> x0, blocking collectives: 22 us -> none  [from_everyone(): return lax.all_to_all(copies, axis, split_axis=0, concat_axis=0, tiled=True)]
    unnamed x21 -> x56, local copies, waits for them, and re-layouts: 29.3 us -> 50.3 us
    all_to_all x4 -> x5, starting transfers between devices: 20.8 us -> 32.9 us  [from_everyone(): return lax.all_to_all(copies, axis, split_axis=0, concat_axis=0, tiled=True)]
    all_to_all x2 -> x0, local copies, waits for them, and re-layouts: 8.47 us -> none  [local(): lax.all_to_all(narrow_down, 'zero', split_axis=1, concat_axis=2, tiled=True)]
    reshape x0 -> x2, local copies, waits for them, and re-layouts: none -> 8.47 us  [local(): jnp.concatenate(lax.all_to_all(jnp.stack(jnp.split(narrow_down, lax.axis_...]
    unnamed x2 -> x1, other arithmetic: 6.73 us -> 2.88 us
    convert_element_type x0 -> x1, other arithmetic: none -> 2.88 us  [local(): (master_down / jnp.expand_dims(scale_down, 2)).astype(jnp.bfloat16)]
    all_to_all x4 -> x5, waiting for transfers between devices: 41.8 us -> 42.3 us  [from_everyone(): return lax.all_to_all(copies, axis, split_axis=0, concat_axis=0, tiled=True)]
  transfers between devices with their start and end apart: 6 -> 7, of which waited for: 6 -> 6; matrix products, arithmetic and copies ran while one was open for 23% -> 32% of each run, Pallas kernels for 0% -> 0%
where the time goes in v1:
time: 226 us; the launch traced here: 225 us
  waiting for transfers between devices  83.1 us (37%)
  local copies, waits for them, and re-layouts  78.7 us (35%)
  starting transfers between devices  44.7 us (20%)
  other arithmetic  17.2 us (8%)
    unnamed x56, local copies, waits for them, and re-layouts  50.3 us
    all_to_all x5, waiting for transfers between devices, from_everyone(): return lax.all_to_all(copies, axis, split_axis=0, concat_axis=0, tiled=True)  42.3 us
    all_to_all x1, waiting for transfers between devices, sent_together(): lax.all_to_all(both, axis, split_axis=split_dim, concat_axis=concat_dim,...  37.1 us
    all_to_all x5, starting transfers between devices, from_everyone(): return lax.all_to_all(copies, axis, split_axis=0, concat_axis=0, tiled=True)  32.9 us
    slice x5, local copies, waits for them, and re-layouts, sent_together(): lax.slice_in_dim(whole, at, at + a.shape[along], axis=along)  10.1 us
    reshape x2, local copies, waits for them, and re-layouts, local(): jnp.concatenate(lax.all_to_all(jnp.stack(jnp.split(narrow_down, lax.axis_...  8.47 us
    convert_element_type x1, other arithmetic, local(): (master_up / jnp.expand_dims(scale_up, 1)).astype(jnp.bfloat16)  6.19 us
    all_to_all x1, starting transfers between devices, sent_together(): lax.all_to_all(both, axis, split_axis=split_dim, concat_axis=concat_dim,...  5.97 us
  transfers between devices with their start and end apart: 7, of which 6 were waited for; matrix products, arithmetic and copies ran while one was open for 32% of the time, Pallas kernels for 0%

profile of v1, /device:TPU:1, one launch (start us, length us, event | category | flops | bytes accessed | tf_op | source)
XLA Modules:
  0.0 224.6 jit_solution(9869695012994616359)
XLA Ops:
  0.6 0.8 multiply_convert_fusion
  1.5 0.7 reshape.46
  2.2 12.6 %all-to-all-start.5 = ((bf16[32,2,256]{2,1,0:T(2,128)(2,1)}), bf16[32,2,256]{2,1,0:T(2,128)(2,1)S(1)}, u32[]{:S(2)}, u32[]{:S(2)}) async-start(bf16[32,2,256]{2,1,0:T(2,128)(2,1)} %reshape.46), calls=%async_computation.5 | async-start | bytes 65536 | tf_op jit(solution)/shard_map/all_to_all | solution.py:9
  14.8 1.9 multiply_reduce_fusion
  16.7 7.8 %all-to-all-done.5 = bf16[32,2,256]{2,1,0:T(2,128)(2,1)S(1)} async-done(((bf16[32,2,256]{2,1,0:T(2,128)(2,1)}), bf16[32,2,256]{2,1,0:T(2,128)(2,1)S(1)}, u32[]{:S(2)}, u32[]{:S(2)}) %all-to-all-start.5) | async-done | bytes 32800 | tf_op jit(solution)/shard_map/all_to_all | solution.py:9
  24.4 0.9 broadcast_in_dim.21
  25.3 3.9 %all-to-all-start.3 = ((bf16[32,8,1024]{2,1,0:T(8,128)(2,1)}), bf16[32,8,1024]{2,1,0:T(8,128)(2,1)S(1)}, u32[]{:S(2)}, u32[]{:S(2)}) async-start(bf16[32,8,1024]{2,1,0:T(8,128)(2,1)} %broadcast_in_dim.21), calls=%async_computation.3 | async-start | bytes 1048576 | tf_op jit(solution)/shard_map/all_to_all | solution.py:9
  29.3 2.7 %copy.47 = f32[8,1024,64]{2,1,0:T(8,128)} copy(f32[8,1024,64]{1,2,0:T(8,128)S(1)} %copy-done) | data formatting | bytes 4194304 | tf_op args[2]
  32.0 2.0 multiply_reduce_fusion.1
  34.7 11.8 %all-to-all-done.3 = bf16[32,8,1024]{2,1,0:T(8,128)(2,1)S(1)} async-done(((bf16[32,8,1024]{2,1,0:T(8,128)(2,1)}), bf16[32,8,1024]{2,1,0:T(8,128)(2,1)S(1)}, u32[]{:S(2)}, u32[]{:S(2)}) %all-to-all-start.3) | async-done | bytes 524320 | tf_op jit(solution)/shard_map/all_to_all | solution.py:9
  46.5 0.7 broadcast_in_dim.23
  47.3 4.2 %all-to-all-start.6 = ((bf16[8,2048,8]{1,2,0:T(8,128)(2,1)}), bf16[8,2048,8]{1,2,0:T(8,128)(2,1)S(1)}, u32[]{:S(2)}, u32[]{:S(2)}) async-start(bf16[8,2048,8]{1,2,0:T(8,128)(2,1)} %broadcast_in_dim.23), calls=%async_computation.6 | async-start | bytes 524288 | tf_op jit(solution)/shard_map/all_to_all | solution.py:9
  51.6 2.9 %divide_convert_fusion = bf16[8,1024,64]{2,1,0:T(8,128)(2,1)S(1)} fusion(f32[8,1024,64]{2,1,0:T(8,128)} %copy.47, f32[8,1024]{1,0:T(8,128)S(1)} %sqrt.23), kind=kLoop, calls=%fused_computation.1 | loop fusion | flops 1048576 | bytes 3178496 | tf_op jit(solution)/shard_map/convert_element_type | solution.py:59
  56.3 0.6 constant_dynamic-update-slice_fusion.28
  62.6 0.6 constant_dynamic-update-slice_fusion.18
  63.8 0.6 constant_dynamic-update-slice_fusion.16
  65.7 0.6 constant_dynamic-update-slice_fusion.13
  68.2 0.9 broadcast_in_dim.20
  69.1 6.4 %all-to-all-start.1 = ((bf16[32,8,1024]{2,1,0:T(8,128)(2,1)}), bf16[32,8,1024]{2,1,0:T(8,128)(2,1)S(1)}, u32[]{:S(2)}, u32[]{:S(2)}) async-start(bf16[32,8,1024]{2,1,0:T(8,128)(2,1)} %broadcast_in_dim.20), calls=%async_computation.1 | async-start | bytes 1048576 | tf_op jit(solution)/shard_map/all_to_all | solution.py:9
  78.6 13.7 %all-to-all-done.1 = bf16[32,8,1024]{2,1,0:T(8,128)(2,1)S(1)} async-done(((bf16[32,8,1024]{2,1,0:T(8,128)(2,1)}), bf16[32,8,1024]{2,1,0:T(8,128)(2,1)S(1)}, u32[]{:S(2)}, u32[]{:S(2)}) %all-to-all-start.1) | async-done | bytes 524320 | tf_op jit(solution)/shard_map/all_to_all | solution.py:9
  92.3 0.9 broadcast_in_dim.19
  93.2 5.8 %all-to-all-start = ((bf16[32,8,1024]{2,1,0:T(8,128)(2,1)}), bf16[32,8,1024]{2,1,0:T(8,128)(2,1)S(1)}, u32[]{:S(2)}, u32[]{:S(2)}) async-start(bf16[32,8,1024]{2,1,0:T(8,128)(2,1)} %broadcast_in_dim.19), calls=%async_computation | async-start | bytes 1048576 | tf_op jit(solution)/shard_map/all_to_all | solution.py:9
  102.2 4.8 %reshape.44 = bf16[32,2,8192]{2,1,0:T(2,128)(2,1)} reshape(bf16[32,8,32,64]{3,2,1,0:T(8,128)(2,1)} %constant_dynamic-update-slice_fusion) | data formatting | bytes 2097152
  107.0 8.9 %all-to-all-done = bf16[32,8,1024]{2,1,0:T(8,128)(2,1)S(1)} async-done(((bf16[32,8,1024]{2,1,0:T(8,128)(2,1)}), bf16[32,8,1024]{2,1,0:T(8,128)(2,1)S(1)}, u32[]{:S(2)}, u32[]{:S(2)}) %all-to-all-start) | async-done | bytes 524320 | tf_op jit(solution)/shard_map/all_to_all | solution.py:9
  115.9 0.8 copy-done.5
  116.7 5.8 %all-to-all-start.4 = ((bf16[32,2,8192]{2,1,0:T(2,128)(2,1)}), bf16[32,2,8192]{2,1,0:T(2,128)(2,1)S(1)}, u32[]{:S(2)}, u32[]{:S(2)}) async-start(bf16[32,2,8192]{2,1,0:T(2,128)(2,1)} %reshape.44), calls=%async_computation.4 | async-start | bytes 2097152 | tf_op jit(solution)/shard_map/all_to_all | solution.py:63
  122.5 2.7 %copy.43 = f32[8,64,1024]{1,0,2:T(8,128)} copy(f32[8,64,1024]{2,1,0:T(8,128)S(1)} %copy-done.1) | data formatting | bytes 4194304 | tf_op args[1]
  125.3 3.9 %copy.41 = f32[8,64,1024]{1,0,2:T(8,128)} copy(f32[8,64,1024]{2,1,0:T(8,128)} %param.5) | data formatting | bytes 4194304 | tf_op args[0]
  129.8 6.2 %divide_convert_fusion.1 = (bf16[8,64,1024]{1,0,2:T(8,128)(2,1)S(1)}, bf16[8,64,1024]{1,0,2:T(8,128)(2,1)S(1)}) fusion(f32[8,64,1024]{1,0,2:T(8,128)} %copy.43, f32[8,1024]{0,1:T(8,128)S(1)} %copy.42, f32[8,64,1024]{1,0,2:T(8,128)} %copy.41, f32[8,1024]{0,1:T(8,128)S(1)} %copy.40), kind=kLoop, calls=%fused_computation.2 | loop fusion | flops 2097152 | bytes 6356992 | tf_op jit(solution)/shard_map/convert_element_type | solution.py:58
  136.0 2.9 %fusion.1 = bf16[1024,16,64]{2,1,0:T(8,128)(2,1)} fusion(bf16[8,64,1024]{1,0,2:T(8,128)(2,1)S(1)} %get-tuple-element.9, bf16[8,64,1024]{1,0,2:T(8,128)(2,1)S(1)} %get-tuple-element.10), kind=kLoop, calls=%fused_computation.79 | loop fusion | flops 4194304 | bytes 4194304
  138.9 7.9 %reshape.42 = bf16[32,2,16384]{2,1,0:T(2,128)(2,1)} reshape(bf16[1024,16,64]{2,1,0:T(8,128)(2,1)} %fusion.1) | data formatting | bytes 4194304
  146.8 3.8 %all-to-all-done.4 = bf16[32,2,8192]{2,1,0:T(2,128)(2,1)S(1)} async-done(((bf16[32,2,8192]{2,1,0:T(2,128)(2,1)}), bf16[32,2,8192]{2,1,0:T(2,128)(2,1)S(1)}, u32[]{:S(2)}, u32[]{:S(2)}) %all-to-all-start.4) | async-done | bytes 1048608 | tf_op jit(solution)/shard_map/all_to_all | solution.py:63
  150.6 6.0 %all-to-all-start.2 = ((bf16[32,2,16384]{2,1,0:T(2,128)(2,1)}), bf16[32,2,16384]{2,1,0:T(2,128)(2,1)S(1)}, u32[]{:S(2)}, u32[]{:S(2)}) async-start(bf16[32,2,16384]{2,1,0:T(2,128)(2,1)} %reshape.42), calls=%async_computation.2 | async-start | bytes 4194304 | tf_op jit(solution)/shard_map/all_to_all | solution.py:20
  156.6 0.7 constant_dynamic-slice_fusion.2
  157.2 0.7 constant_dynamic-slice_fusion.1
  157.9 0.7 constant_dynamic-slice_fusion
  158.6 2.4 %reshape.45 = bf16[32,8,32,64]{3,2,1,0:T(8,128)(2,1)} reshape(bf16[32,2,8192]{2,1,0:T(2,128)(2,1)S(1)} %all-to-all-done.4) | data formatting | bytes 2097152
  160.9 4.2 %copy.48 = bf16[8,32,32,64]{3,2,1,0:T(8,128)(2,1)} copy(bf16[8,32,32,64]{3,1,0,2:T(8,128)(2,1)} %bitcast.155) | data formatting | bytes 2097152 | tf_op jit(solution)/shard_map/reshape | solution.py:62
  165.2 4.2 %reshape.39 = bf16[8,32,2048]{2,1,0:T(8,128)(2,1)} reshape(bf16[8,32,32,64]{3,2,1,0:T(8,128)(2,1)} %copy.48) | data formatting | bytes 2097152 | tf_op jit(solution)/shard_map/reshape | solution.py:62
  169.4 37.1 %all-to-all-done.2 = bf16[32,2,16384]{2,1,0:T(2,128)(2,1)S(1)} async-done(((bf16[32,2,16384]{2,1,0:T(2,128)(2,1)}), bf16[32,2,16384]{2,1,0:T(2,128)(2,1)S(1)}, u32[]{:S(2)}, u32[]{:S(2)}) %all-to-all-start.2) | async-done | bytes 2097184 | tf_op jit(solution)/shard_map/all_to_all | solution.py:20
  206.5 4.0 %reshape.43 = bf16[1024,16,64]{2,1,0:T(8,128)(2,1)} reshape(bf16[32,2,16384]{2,1,0:T(2,128)(2,1)S(1)} %all-to-all-done.2) | data formatting | bytes 4194304
  210.5 3.3 %copy.44 = bf16[16,64,1024]{1,2,0:T(8,128)(2,1)S(1)} copy(bf16[16,64,1024]{1,0,2:T(8,128)(2,1)} %bitcast.154) | data formatting | bytes 4194304 | tf_op jit(solution)/shard_map/all_to_all | solution.py:20
  213.7 2.1 fusion
  215.8 0.8 copy.45
  216.6 2.4 %slice.13 = bf16[8,2048,32]{1,2,0:T(8,128)(2,1)} reshape(bf16[8,32,64,32]{2,1,3,0:T(8,128)(2,1)S(1)} %copy.45) | data formatting | bytes 2097152 | tf_op jit(solution)/shard_map/slice | solution.py:25
  219.0 2.4 %copy.46 = bf16[8,32,64,32]{2,1,3,0:T(8,128)(2,1)S(1)} copy(bf16[8,32,64,32]{2,3,1,0:T(8,128)(2,1)} %get-tuple-element.7) | data formatting | bytes 2097152 | tf_op jit(solution)/shard_map/slice | solution.py:25
  221.4 2.4 %slice.15 = bf16[8,2048,32]{1,2,0:T(8,128)(2,1)} reshape(bf16[8,32,64,32]{2,1,3,0:T(8,128)(2,1)S(1)} %copy.46) | data formatting | bytes 2097152 | tf_op jit(solution)/shard_map/slice | solution.py:25
  223.9 0.7 copy.82
  (55 shorter events, 18.9 us)
Async XLA Ops:
  0.6 28.6 %copy-start = (f32[8,1024,64]{1,2,0:T(8,128)S(1)}, f32[8,1024,64]{1,2,0:T(8,128)}, u32[]{:S(2)}) copy-start(f32[8,1024,64]{1,2,0:T(8,128)} %param.7) | copy-start | bytes 6291460
  2.2 22.2 %all-to-all-start.5 = ((bf16[32,2,256]{2,1,0:T(2,128)(2,1)}), bf16[32,2,256]{2,1,0:T(2,128)(2,1)S(1)}, u32[]{:S(2)}, u32[]{:S(2)}) async-start(bf16[32,2,256]{2,1,0:T(2,128)(2,1)} %reshape.46), calls=%async_computation.5 | async-start | bytes 65536 | tf_op jit(solution)/shard_map/all_to_all | solution.py:9
  25.3 21.3 %all-to-all-start.3 = ((bf16[32,8,1024]{2,1,0:T(8,128)(2,1)}), bf16[32,8,1024]{2,1,0:T(8,128)(2,1)S(1)}, u32[]{:S(2)}, u32[]{:S(2)}) async-start(bf16[32,8,1024]{2,1,0:T(8,128)(2,1)} %broadcast_in_dim.21), calls=%async_computation.3 | async-start | bytes 1048576 | tf_op jit(solution)/shard_map/all_to_all | solution.py:9
  32.0 2.2 copy-start.2
  47.3 21.0 %all-to-all-start.6 = ((bf16[8,2048,8]{1,2,0:T(8,128)(2,1)}), bf16[8,2048,8]{1,2,0:T(8,128)(2,1)S(1)}, u32[]{:S(2)}, u32[]{:S(2)}) async-start(bf16[8,2048,8]{1,2,0:T(8,128)(2,1)} %broadcast_in_dim.23), calls=%async_computation.6 | async-start | bytes 524288 | tf_op jit(solution)/shard_map/all_to_all | solution.py:9
  69.1 23.2 %all-to-all-start.1 = ((bf16[32,8,1024]{2,1,0:T(8,128)(2,1)}), bf16[32,8,1024]{2,1,0:T(8,128)(2,1)S(1)}, u32[]{:S(2)}, u32[]{:S(2)}) async-start(bf16[32,8,1024]{2,1,0:T(8,128)(2,1)} %broadcast_in_dim.20), calls=%async_computation.1 | async-start | bytes 1048576 | tf_op jit(solution)/shard_map/all_to_all | solution.py:9
  92.3 14.6 %copy-start.3 = (bf16[32,8,1024]{2,1,0:T(8,128)(2,1)}, bf16[32,8,1024]{2,1,0:T(8,128)(2,1)S(1)}, u32[]{:S(2)}) copy-start(bf16[32,8,1024]{2,1,0:T(8,128)(2,1)S(1)} %all-to-all-done.1) | copy-start | bytes 1572868
  93.2 22.7 %all-to-all-start = ((bf16[32,8,1024]{2,1,0:T(8,128)(2,1)}), bf16[32,8,1024]{2,1,0:T(8,128)(2,1)S(1)}, u32[]{:S(2)}, u32[]{:S(2)}) async-start(bf16[32,8,1024]{2,1,0:T(8,128)(2,1)} %broadcast_in_dim.19), calls=%async_computation | async-start | bytes 1048576 | tf_op jit(solution)/shard_map/all_to_all | solution.py:9
  102.2 20.4 %copy-start.1 = (f32[8,64,1024]{2,1,0:T(8,128)S(1)}, f32[8,64,1024]{2,1,0:T(8,128)}, u32[]{:S(2)}) copy-start(f32[8,64,1024]{2,1,0:T(8,128)} %param.6) | copy-start | bytes 6291460
  115.9 0.8 copy-start.5
  116.7 33.9 %all-to-all-start.4 = ((bf16[32,2,8192]{2,1,0:T(2,128)(2,1)}), bf16[32,2,8192]{2,1,0:T(2,128)(2,1)S(1)}, u32[]{:S(2)}, u32[]{:S(2)}) async-start(bf16[32,2,8192]{2,1,0:T(2,128)(2,1)} %reshape.44), calls=%async_computation.4 | async-start | bytes 2097152 | tf_op jit(solution)/shard_map/all_to_all | solution.py:63
  125.3 4.0 %copy-start.4 = (bf16[32,8,1024]{2,1,0:T(8,128)(2,1)S(1)}, bf16[32,8,1024]{2,1,0:T(8,128)(2,1)}, u32[]{:S(2)}) copy-start(bf16[32,8,1024]{2,1,0:T(8,128)(2,1)} %copy-done.3) | copy-start | bytes 1572868
  125.3 4.3 %copy-start.6 = (bf16[32,8,1024]{2,1,0:T(8,128)(2,1)S(1)}, bf16[32,8,1024]{2,1,0:T(8,128)(2,1)}, u32[]{:S(2)}) copy-start(bf16[32,8,1024]{2,1,0:T(8,128)(2,1)} %copy-done.5) | copy-start | bytes 1572868
  150.6 55.9 %all-to-all-start.2 = ((bf16[32,2,16384]{2,1,0:T(2,128)(2,1)}), bf16[32,2,16384]{2,1,0:T(2,128)(2,1)S(1)}, u32[]{:S(2)}, u32[]{:S(2)}) async-start(bf16[32,2,16384]{2,1,0:T(2,128)(2,1)} %reshape.42), calls=%async_computation.2 | async-start | bytes 4194304 | tf_op jit(solution)/shard_map/all_to_all | solution.py:20
